TPU v7x, 128 devices: a whole 4x4x4 slice. The times are simulated.
128 devices in a mesh: left: 32 (over z, y_lo, x), right: 4 (over y_hi, core).
Axes of the slice: x: 4, y: 4 (y_hi: 2, y_lo: 2; y = y_hi * 2 + y_lo), z: 4, core: 2. Of those that a mesh axis runs over, the one named last changes fastest.
Arguments:
- density: float32 [512, 512, 2048], P(None, 'left', 'right'), may hold values from -6 to 6
- symbol_x: float32 [512], replicated, may hold values from 0.3 to 3
- symbol_y: float32 [512], replicated, may hold values from 0.3 to 3
- symbol_z: float32 [2048], replicated, may hold values from 0.3 to 3
Outputs:
- spectrum: float32 [512, 512, 2048], P('left', 'right')
All inputs are finite; a program needn't handle non-finite values.
Results may differ from a plain program's by a relative error of at most 0.00007.
Values sent between devices are 32-bit elements; how exact they have to be, the bound alone decides.
A program may use at most 192 MiB of HBM per device.

v0:
```python
import jax
import jax.numpy as jnp
from jax import lax
from jax.sharding import PartitionSpec as P


def split_up(x, dim, count):
    shape = x.shape
    parts = x.reshape(*shape[:dim], count, shape[dim] // count, *shape[dim + 1 :])
    return jnp.moveaxis(parts, dim, 0)


def edges_of(length, count):
    hop = length // count
    if hop >= 8:
        hop -= hop % 8
    return [hop * k for k in range(1, count)]


def joined_along(parts, dim):
    parts = jnp.moveaxis(parts, 0, dim)
    shape = parts.shape
    return parts.reshape(*shape[:dim], shape[dim] * shape[dim + 1], *shape[dim + 2 :])


def several_exchanges(x, axis, pieces, split_dim, concat_dim):
    parts = split_up(x, split_dim, lax.axis_size(axis))
    split_at = max(range(1, max(2, parts.ndim - 1)), key=lambda d: parts.shape[d])
    gathered = []
    for section in jnp.split(parts, edges_of(parts.shape[split_at], pieces), axis=split_at):
        if section.size:
            gathered.append(lax.all_to_all(section, axis, split_axis=0, concat_axis=0, tiled=True))
    return joined_along(jnp.concatenate(gathered, axis=split_at), concat_dim)


def mode_table(count):
    rank = jnp.arange(count)
    angle = 2.0 * jnp.pi / count * (rank[:, None] * rank[None, :] % count).astype(jnp.float32)
    return (jnp.cos(angle) + jnp.sin(angle)) * count ** (-0.5)


def transform_dim(values, dim):
    moved = jnp.tensordot(
        values, mode_table(values.shape[dim]), axes=([dim], [0]), precision=lax.Precision.HIGHEST
    )
    return jnp.moveaxis(moved, -1, dim)


def per_device(density, symbol_x, symbol_y, symbol_z):
    part_values = density
    part_values = transform_dim(part_values, 0)
    part_values = lax.all_to_all(part_values, "left", split_axis=0, concat_axis=1, tiled=True)
    part_values = transform_dim(part_values, 1)
    block_values = part_values
    block_values = several_exchanges(block_values, "right", 2, 1, 2)
    block_values = transform_dim(block_values, 2)
    share_x = block_values.shape[0]
    part_x = lax.dynamic_slice_in_dim(symbol_x, lax.axis_index("left") * share_x, share_x)
    share_y = block_values.shape[1]
    part_y = lax.dynamic_slice_in_dim(symbol_y, lax.axis_index("right") * share_y, share_y)
    symbol = part_x[:, None, None] + part_y[None, :, None] + symbol_z[None, None, :]
    block_values = block_values * lax.rsqrt(symbol)
    return block_values


def solution(mesh):
    return jax.shard_map(
        per_device,
        mesh=mesh,
        in_specs=(P(None, "left", "right"), P(), P(), P()),
        out_specs=P("left", "right", None),
        check_vma=False,
    )
```

profile of v0, /device:TPU:1, one launch (start us, length us, event | category | flops | bytes accessed | tf_op | source)
XLA Modules:
  0.0 652.0 jit_solution(314109085938783773)
XLA Ops:
  0.0 4.2 fusion.57
  4.2 38.0 %fusion.5 = f32[512,16,512]{2,0,1:T(8,128)S(1)} fusion(f32[512,16,512]{2,1,0:T(8,128)} %param.4, f32[512,512,1]{0,1,2:T(8,128)S(1)} %fusion.57), kind=kOutput, calls=%fused_computation.10 | convolution fusion | flops 25769803776 | bytes 34603008 | tf_op jit(solution)/shard_map/dot_general | solution.py:43
  42.2 17.2 %copy.9 = f32[512,16,512]{2,1,0:T(8,128)S(1)} copy(f32[512,16,512]{2,0,1:T(8,128)S(1)} %fusion.5) | data formatting | bytes 33554432 | tf_op jit(solution)/shard_map/dot_general | solution.py:43
  59.4 193.5 %all_to_all.28 = f32[512,16,512]{2,1,0:T(8,128)S(1)} all-to-all(f32[512,16,512]{2,1,0:T(8,128)S(1)} %copy.9), channel_id=1, replica_groups=mesh['left'=32,'right'=4] {'left'}, dimensions={0} | all-to-all | bytes 33554432 | tf_op jit(solution)/shard_map/all_to_all | solution.py:52
  252.9 6.4 copy.10
  259.3 44.4 %fusion.27 = f32[16,512,512]{1,2,0:T(8,128)} fusion(f32[16,512,512]{2,1,0:T(8,128)} %bitcast.37), kind=kOutput, calls=%fused_computation.31 | convolution fusion | flops 25773998080 | bytes 33554432 | tf_op jit(solution)/shard_map/dot_general | solution.py:43
  303.8 7.0 %copy.18 = f32[16,4,128,512]{3,2,0,1:T(8,128)S(1)} copy(f32[16,4,128,512]{3,2,1,0:T(8,128)} %bitcast.38) | data formatting | bytes 33554432 | tf_op jit(solution)/shard_map/reshape | solution.py:9
  310.7 6.9 %fusion.48 = (f32[4,16,64,512]{3,2,1,0:T(8,128)}, f32[4,16,64,512]{3,2,1,0:T(8,128)}) fusion(f32[4,16,128,512]{3,2,1,0:T(8,128)S(1)} %bitcast.35), kind=kLoop, calls=%fused_computation.54 | loop fusion | bytes 33554432 | tf_op jit(solution)/shard_map/split | solution.py:30
  317.7 103.2 %all_to_all.29 = f32[4,16,64,512]{3,2,1,0:T(8,128)} all-to-all(f32[4,16,64,512]{3,2,1,0:T(8,128)} %get-tuple-element.5), channel_id=1, replica_groups=mesh['left'=32,'right'=4] {'right'}, dimensions={0} | all-to-all | bytes 16777216 | tf_op jit(solution)/shard_map/all_to_all | solution.py:32
  420.9 6.6 %all-to-all-start.2 = ((f32[4,16,64,512]{3,2,1,0:T(8,128)}), f32[4,16,64,512]{3,2,1,0:T(8,128)}, u32[]{:S(2)}, u32[]{:S(2)}) async-start(f32[4,16,64,512]{3,2,1,0:T(8,128)} %get-tuple-element.6), calls=%async_computation.2 | async-start | bytes 16777216 | tf_op jit(solution)/shard_map/all_to_all | solution.py:32
  427.5 0.8 dynamic_slice.7
  428.3 0.8 dynamic_slice.6
  429.0 0.1 broadcast_add_fusion
  429.1 67.7 %fusion.59 = f32[2048,2048,1]{1,0,2:T(8,128)} fusion(), kind=kLoop, calls=%fused_computation.8.clone.clone.clone.1 | loop fusion | flops 67108864 | bytes 16777216 | tf_op jit(solution)/shard_map/dot_general | solution.py:43
  496.8 24.5 %all-to-all-done.2 = f32[4,16,64,512]{3,2,1,0:T(8,128)} async-done(((f32[4,16,64,512]{3,2,1,0:T(8,128)}), f32[4,16,64,512]{3,2,1,0:T(8,128)}, u32[]{:S(2)}, u32[]{:S(2)}) %all-to-all-start.2) | async-done | bytes 8388640 | tf_op jit(solution)/shard_map/all_to_all | solution.py:32
  521.3 6.9 %maximum_bitcast_fusion = f32[4,16,16,8,512]{4,3,2,1,0:T(8,128)S(1)} fusion(f32[4,16,64,512]{3,2,1,0:T(8,128)} %all-to-all-done.2, f32[4,16,64,512]{3,2,1,0:T(8,128)} %all_to_all.29), kind=kLoop, calls=%fused_computation.6 | loop fusion | flops 4194304 | bytes 33554432
  528.2 0.0 copy-start
  528.2 6.2 copy.13
  534.4 0.0 copy-done
  534.4 117.4 %rsqrt_multiply_fusion = f32[16,128,2048]{2,1,0:T(8,128)} fusion(f32[2048]{0:T(1024)S(1)} %copy-done, f32[16,128]{1,0:T(8,128)S(1)} %broadcast_add_fusion, f32[16,128,2048]{2,1,0:T(8,128)} %bitcast.39, f32[2048,2048,1]{1,0,2:T(8,128)} %fusion.59), kind=kOutput, calls=%fused_computation.12 | convolution fusion | flops 103087603712 | bytes 50348032 | tf_op jit(solution)/shard_map/dot_general | solution.py:43
Async XLA Ops:
  420.9 100.4 %all-to-all-start.2 = ((f32[4,16,64,512]{3,2,1,0:T(8,128)}), f32[4,16,64,512]{3,2,1,0:T(8,128)}, u32[]{:S(2)}, u32[]{:S(2)}) async-start(f32[4,16,64,512]{3,2,1,0:T(8,128)} %get-tuple-element.6), calls=%async_computation.2 | async-start | bytes 16777216 | tf_op jit(solution)/shard_map/all_to_all | solution.py:32
  528.2 6.2 copy-start
where the time goes:
time: 662 us; the launch traced here: 652 us
  blocking collectives  297 us (45%)
  matrix products  200 us (30%)
  other arithmetic  78.8 us (12%)
  local copies, waits for them, and re-layouts  45.2 us (7%)
  waiting for transfers between devices  24.5 us (4%)
  starting transfers between devices  6.63 us (1%)
    dot_general x3, matrix products, transform_dim(): jnp.tensordot(values, mode_table(values.shape[dim]), axes=([dim], [0]), p...  200 us
    all_to_all x1, blocking collectives, per_device(): lax.all_to_all(part_values, 'left', split_axis=0, concat_axis=1, tiled=True)  194 us
    all_to_all x1, blocking collectives, several_exchanges(): lax.all_to_all(section, axis, split_axis=0, concat_axis=0, tiled=True)  103 us
    dot_general x2, other arithmetic, transform_dim(): jnp.tensordot(values, mode_table(values.shape[dim]), axes=([dim], [0]), p...  71.8 us
    all_to_all x1, waiting for transfers between devices, several_exchanges(): lax.all_to_all(section, axis, split_axis=0, concat_axis=0, tiled=True)  24.5 us
    dot_general x1, local copies, waits for them, and re-layouts, transform_dim(): jnp.tensordot(values, mode_table(values.shape[dim]), axes=([dim], [0]), p...  17.2 us
  transfers between devices with their start and end apart: 1, of which 1 were waited for; matrix products, arithmetic and copies ran while one was open for 11% of the time, Pallas kernels for 0%

commit v1 on v0

v1 whole, which is shorter than its diff:
```python
import jax
import jax.numpy as jnp
import numpy as np
from jax import lax
from jax.experimental import pallas as pl
from jax.experimental.pallas import tpu as pltpu
from jax.sharding import PartitionSpec as P

MESH = pl.DeviceIdType.MESH
F32 = jnp.float32
BF16 = jnp.bfloat16
LANES = 128


def halves(value):
    high = value.astype(BF16)
    return high, (value - high.astype(F32)).astype(BF16)


def small_table(count):
    rank = np.arange(count)
    angle = 2.0 * np.pi / count * (rank[:, None] * rank[None, :] % count)
    table = ((np.cos(angle) + np.sin(angle)) * count ** (-0.5)).astype(np.float32)
    high = table.astype(BF16)
    low = (table - high.astype(np.float32)).astype(BF16)
    return np.stack([high, low])


def factor_tables(count, inner):
    rest, col = np.arange(inner), np.arange(count)
    angle = 2.0 * np.pi / count * (rest[:, None] * col[None, :] % count)
    scale = count ** (-0.5)
    plus = (np.cos(angle) + np.sin(angle)) * scale
    minus = (np.cos(angle) - np.sin(angle)) * scale
    outer = np.arange(count // inner)
    angle = 2.0 * np.pi / count * (outer[:, None] * inner * np.arange(LANES)[None, :] % count)
    return np.stack([plus, minus]).astype(np.float32), np.stack([np.cos(angle), np.sin(angle)]).astype(np.float32)


def dot(a, b):
    return jnp.dot(a, b, preferred_element_type=F32)


def make_kernel(n_left, n_right, size_x, size_y, size_z):
    part_x, part_y, rows_y, part_z = size_x // n_left, size_y // n_left, size_y // n_right, size_z // n_right
    inner = 64

    def partner(me, step):
        x = step & 3
        k = step >> 2
        z = (k ^ x) & 3
        y = ((k >> 2) ^ (x >> 1)) & 1
        return me ^ ((z << 3) | (y << 2) | x)

    def kernel(
        field, small, cas, turn,
        lines_y, lines_z, result,
        held, big_high, big_low, taken, stacked, given,
        load_sem, send_x, recv_x, keep_x, send_y, recv_y, keep_y, z_in_sem, z_out_sem,
    ):
        left = lax.axis_index("left")
        right = lax.axis_index("right")

        def load_x(y, slot):
            return pltpu.make_async_copy(field.at[:, y, :], taken.at[slot], load_sem.at[slot])

        load_x(0, 0).start()

        barrier = pltpu.get_barrier_semaphore()

        @pl.loop(1, n_left)
        def _(step):
            pl.semaphore_signal(barrier, inc=1, device_id={"left": partner(left, step)}, device_id_type=MESH)

        @pl.loop(1, n_right)
        def _(step):
            pl.semaphore_signal(barrier, inc=1, device_id={"right": right ^ step}, device_id_type=MESH)

        pl.semaphore_wait(barrier, n_left + n_right - 2)

        def transform(slot, out):
            for n in range(0, part_z, 256):
                high, low = halves(taken[slot, :, n : n + 256])
                held[out, :, n : n + 256] = dot(small[0], high) + dot(small[0], low) + dot(small[1], high)

        @pl.loop(0, part_y)
        def _(y):
            slot = y & 1

            @pl.when(y + 1 < part_y)
            def _():
                load_x(y + 1, 1 - slot).start()

            load_x(y, slot).wait()
            transform(slot, y)
            to = left * part_y + y

            @pl.loop(1, n_left)
            def _(step):
                peer = partner(left, step)
                pltpu.make_async_remote_copy(
                    src_ref=held.at[y, pl.ds(peer * part_x, part_x)],
                    dst_ref=lines_y.at[to],
                    send_sem=send_x,
                    recv_sem=recv_x,
                    device_id={"left": peer},
                    device_id_type=MESH,
                ).start()

            pltpu.make_async_copy(held.at[y, pl.ds(left * part_x, part_x)], lines_y.at[to], keep_x).start()

        @pl.loop(0, size_z // inner)
        def _(outer):
            cos = turn[0, pl.ds(outer, 1), :]
            sin = turn[1, pl.ds(outer, 1), :]
            for c in range(0, size_z, LANES):
                value = cas[0, :, c : c + LANES] * cos + cas[1, :, c : c + LANES] * sin
                high, low = halves(value)
                big_high[pl.ds(outer * inner, inner), c : c + LANES] = high
                big_low[pl.ds(outer * inner, inner), c : c + LANES] = low

        own = lines_y.at[pl.ds(0, part_y)]
        pltpu.make_async_copy(own, own, keep_x).wait()
        others = lines_y.at[pl.ds(0, size_y - part_y)]
        pltpu.make_async_copy(others, others, send_x).wait()
        pltpu.make_async_copy(others, others, recv_x).wait()

        def load_y(k, slot):
            return pltpu.make_async_copy(lines_y.at[:, k, :], taken.at[slot], load_sem.at[slot])

        load_y(0, 0).start()

        @pl.loop(0, part_x)
        def _(k):
            slot = k & 1

            @pl.when(k + 1 < part_x)
            def _():
                load_y(k + 1, 1 - slot).start()

            load_y(k, slot).wait()
            transform(slot, k)
            columns = pl.ds(pl.multiple_of(right * part_z, part_z), part_z)

            @pl.loop(0, n_right - 1)
            def _(step):
                peer = right ^ lax.rem(step + 1, n_right - 1) + 1
                pltpu.make_async_remote_copy(
                    src_ref=held.at[k, pl.ds(peer * rows_y, rows_y)],
                    dst_ref=lines_z.at[k, :, columns],
                    send_sem=send_y,
                    recv_sem=recv_y.at[k],
                    device_id={"right": peer},
                    device_id_type=MESH,
                ).start()

            pltpu.make_async_copy(held.at[k, pl.ds(right * rows_y, rows_y)], lines_z.at[k, :, columns], keep_y.at[k]).start()

        def store_z(k, slot):
            return pltpu.make_async_copy(given.at[slot], result.at[k], z_out_sem.at[slot])

        @pl.loop(0, part_x)
        def _(k):
            slot = k & 1
            mine = lines_z.at[k, :, pl.ds(0, part_z)]
            pltpu.make_async_copy(mine, mine, keep_y.at[k]).wait()
            theirs = lines_z.at[k, :, pl.ds(0, size_z - part_z)]
            pltpu.make_async_copy(theirs, theirs, recv_y.at[k]).wait()
            for r in range(n_right):
                pltpu.make_async_copy(
                    lines_z.at[k, :, pl.ds(r * part_z, part_z)], taken.at[0, pl.ds(r * rows_y, rows_y)], z_in_sem.at[r]
                ).start()
            for r in range(n_right):
                pltpu.make_async_copy(
                    lines_z.at[k, :, pl.ds(r * part_z, part_z)], taken.at[0, pl.ds(r * rows_y, rows_y)], z_in_sem.at[r]
                ).wait()
                high, low = halves(taken[0, r * rows_y : (r + 1) * rows_y, :])
                stacked[:rows_y, r * part_z : (r + 1) * part_z] = high
                stacked[rows_y:, r * part_z : (r + 1) * part_z] = low

            @pl.when(k >= 2)
            def _():
                store_z(k - 2, slot).wait()

            @pl.loop(0, size_z, step=256)
            def _(n):
                cut = pl.ds(pl.multiple_of(n, 256), 256)
                both = dot(stacked[...], big_high[:, cut])
                given[slot, :, cut] = both[:rows_y] + both[rows_y:] + dot(stacked[:rows_y, :], big_low[:, cut])

            store_z(k, slot).start()

        for k in (part_x - 2, part_x - 1):
            store_z(k, k & 1).wait()
        sent = result.at[pl.ds(0, part_x), :, pl.ds(0, size_z - part_z)]
        pltpu.make_async_copy(sent, sent, send_y).wait()

    held_rows = max(part_x, part_y)
    anywhere = pl.BlockSpec(memory_space=pl.ANY)
    inside = pl.BlockSpec(memory_space=pltpu.VMEM)
    dma = pltpu.SemaphoreType.DMA
    return pl.pallas_call(
        kernel,
        out_shape=[
            jax.ShapeDtypeStruct((size_y, part_x, part_z), F32),
            jax.ShapeDtypeStruct((part_x, rows_y, size_z), F32),
            jax.ShapeDtypeStruct((part_x, rows_y, size_z), F32),
        ],
        in_specs=[anywhere, inside, inside, inside],
        out_specs=[anywhere] * 3,
        scratch_shapes=[
            pltpu.VMEM((held_rows, size_x, part_z), F32),
            pltpu.VMEM((size_z, size_z), BF16),
            pltpu.VMEM((size_z, size_z), BF16),
            pltpu.VMEM((2, size_x, part_z), F32),
            pltpu.VMEM((2 * rows_y, size_z), BF16),
            pltpu.VMEM((2, rows_y, size_z), F32),
            dma((2,)),
            dma, dma, dma,
            dma, dma((part_x,)), dma((part_x,)),
            dma((n_right,)), dma((2,)),
        ],
        compiler_params=pltpu.CompilerParams(
            collective_id=0, has_side_effects=True, vmem_limit_bytes=62 * 1024 * 1024
        ),
        name="hartley",
    )


def solution(mesh):
    n_left, n_right = mesh.shape["left"], mesh.shape["right"]

    def per_device(density, symbol_x, symbol_y, symbol_z):
        size_x, size_y, size_z = density.shape[0], density.shape[1] * n_left, density.shape[2] * n_right
        small = jnp.asarray(small_table(size_x))
        cas, turn = (jnp.asarray(t) for t in factor_tables(size_z, 64))
        result = make_kernel(n_left, n_right, size_x, size_y, size_z)(density, small, cas, turn)[2]
        share_x, share_y = size_x // n_left, size_y // n_right
        part_x = lax.dynamic_slice_in_dim(symbol_x, lax.axis_index("left") * share_x, share_x)
        part_y = lax.dynamic_slice_in_dim(symbol_y, lax.axis_index("right") * share_y, share_y)
        symbol = part_x[:, None, None] + part_y[None, :, None] + symbol_z[None, None, :]
        return result * lax.rsqrt(symbol)

    return jax.shard_map(
        per_device,
        mesh=mesh,
        in_specs=(P(None, "left", "right"), P(), P(), P()),
        out_specs=P("left", "right", None),
        check_vma=False,
    )
```

time: 662 us -> 404 us (0.61)
  Pallas kernels: 0 us -> 385 us
  blocking collectives: 297 us -> 0 us
  matrix products: 200 us -> 0 us
  other arithmetic: 78.8 us -> 12.1 us
  local copies, waits for them, and re-layouts: 45.2 us -> 1.52 us
  waiting for transfers between devices: 24.5 us -> 0 us
  starting transfers between devices: 6.63 us -> 0 us
    pallas_call x0 -> x1, Pallas kernels: none -> 385 us  [per_device(): make_kernel(n_left, n_right, size_x, size_y, size_z)]
    all_to_all x2 -> x0, blocking collectives: 297 us -> none  [the longest x1 194 us: per_device(): lax.all_to_all(part_values, 'left', split_axis=0, concat_axis=1, tiled=True)]
    dot_general x3 -> x0, matrix products: 200 us -> none  [transform_dim(): jnp.tensordot(values, mode_table(values.shape[dim]), axes=([dim], [0]), p...]
    dot_general x2 -> x0, other arithmetic: 71.8 us -> none  [transform_dim(): jnp.tensordot(values, mode_table(values.shape[dim]), axes=([dim], [0]), p...]
    all_to_all x1 -> x0, waiting for transfers between devices: 24.5 us -> none  [several_exchanges(): lax.all_to_all(section, axis, split_axis=0, concat_axis=0, tiled=True)]
    dot_general x1 -> x0, local copies, waits for them, and re-layouts: 17.2 us -> none  [transform_dim(): jnp.tensordot(values, mode_table(values.shape[dim]), axes=([dim], [0]), p...]
    reshape x2 -> x0, local copies, waits for them, and re-layouts: 13.2 us -> none  [the longest x1 6.95 us: split_up(): x.reshape(*shape[:dim], count, shape[dim] // count, *shape[dim + 1:])]
    mul x0 -> x1, other arithmetic: none -> 12 us  [per_device(): return result * lax.rsqrt(symbol)]
  transfers between devices with their start and end apart: 1 -> 0, of which waited for: 1 -> 0; matrix products, arithmetic and copies ran while one was open for 11% -> 0% of each run, Pallas kernels for 0% -> 0%
where the time goes in v1:
time: 404 us; the launch traced here: 399 us
  Pallas kernels  385 us (95%)
  other arithmetic  12.1 us (3%)
    pallas_call x1, Pallas kernels, per_device(): make_kernel(n_left, n_right, size_x, size_y, size_z)  385 us
    mul x1, other arithmetic, per_device(): return result * lax.rsqrt(symbol)  12 us

profile of v1, /device:TPU:1, one launch (start us, length us, event | category | flops | bytes accessed | tf_op | source)
XLA Modules:
  0.0 398.9 jit_solution(5132845123358509212)
XLA Ops:
  0.0 0.0 copy-start
  0.0 385.2 %hartley.1 = (f32[512,16,512]{2,1,0:T(8,128)}, f32[16,128,2048]{2,1,0:T(8,128)}, f32[16,128,2048]{2,1,0:T(8,128)}) custom-call(f32[512,16,512]{2,1,0:T(8,128)} %field.1, bf16[2,512,512]{2,1,0:T(8,128)(2,1)} %constant.23.clone.small, f32[2,64,2048]{2,1,0:T(8,128)} %constant.24.clone.cas, f32[2,32,128]{2,1,0:T(8,128)} %constant.25.clone.turn), custom_call_target="tpu_custom_call" | custom-call | tf_op jit(solution)/shard_map/hartley/pallas_call | solution.py:237
  385.2 0.8 dynamic_slice.7
  386.0 0.8 dynamic_slice.6
  386.8 0.1 broadcast_add_fusion
  386.8 0.0 copy-done
  386.8 12.0 %rsqrt_multiply_fusion = f32[16,128,2048]{2,1,0:T(8,128)} fusion(f32[16,128,2048]{2,1,0:T(8,128)} %get-tuple-element.6, f32[2048]{0:T(1024)S(1)} %copy-done, f32[16,128]{1,0:T(8,128)S(1)} %broadcast_add_fusion), kind=kLoop, calls=%fused_computation | loop fusion | flops 8388608 | bytes 33570816 | tf_op jit(solution)/shard_map/mul | solution.py:242
Async XLA Ops:
  0.0 386.8 %copy-start = (f32[2048]{0:T(1024)S(1)}, f32[2048]{0:T(1024)}, u32[]{:S(2)}) copy-start(f32[2048]{0:T(1024)} %param.10) | copy-start | bytes 24580

commit v2 on v1

v2 whole, which is shorter than its diff:
```python
import jax
import jax.numpy as jnp
import numpy as np
from jax import lax
from jax.experimental import pallas as pl
from jax.experimental.pallas import tpu as pltpu
from jax.sharding import PartitionSpec as P

MESH = pl.DeviceIdType.MESH
F32 = jnp.float32
BF16 = jnp.bfloat16
LANES = 128


def halves(value):
    high = value.astype(BF16)
    return high, (value - high.astype(F32)).astype(BF16)


def small_table(count):
    rank = np.arange(count)
    angle = 2.0 * np.pi / count * (rank[:, None] * rank[None, :] % count)
    table = ((np.cos(angle) + np.sin(angle)) * count ** (-0.5)).astype(np.float32)
    high = table.astype(BF16)
    low = (table - high.astype(np.float32)).astype(BF16)
    return np.stack([high, low])


def factor_tables(count, inner):
    rest, col = np.arange(inner), np.arange(count)
    angle = 2.0 * np.pi / count * (rest[:, None] * col[None, :] % count)
    scale = count ** (-0.5)
    plus = (np.cos(angle) + np.sin(angle)) * scale
    minus = (np.cos(angle) - np.sin(angle)) * scale
    outer = np.arange(count // inner)
    angle = 2.0 * np.pi / count * (outer[:, None] * inner * np.arange(LANES)[None, :] % count)
    return np.stack([plus, minus]).astype(np.float32), np.stack([np.cos(angle), np.sin(angle)]).astype(np.float32)


def dot(a, b):
    return jnp.dot(a, b, preferred_element_type=F32)


def make_kernel(n_left, n_right, size_x, size_y, size_z):
    part_x, part_y, rows_y, part_z = size_x // n_left, size_y // n_left, size_y // n_right, size_z // n_right
    half_x, half_z = part_x // 2, size_z // 2
    inner = 64

    def partner(me, step):
        x = step & 3
        k = step >> 2
        z = (k ^ x) & 3
        y = ((k >> 2) ^ (x >> 1)) & 1
        return me ^ ((z << 3) | (y << 2) | x)

    def kernel(
        field, small_far, cas_far, turn_far, sym_x, sym_y, sym_z,
        lines_y, lines_z, result,
        held, big_high, big_low, taken, line_in, stacked, partial, small, cas, turn, column,
        load_sem, table_sem, send_x, recv_x, keep_x, send_y, near_y, far_y, keep_y, line_sem,
    ):
        left = lax.axis_index("left")
        right = lax.axis_index("right")

        def load_x(y, slot):
            return pltpu.make_async_copy(field.at[:, y, :], taken.at[slot], load_sem.at[slot])

        tables = [
            pltpu.make_async_copy(far, near, table_sem.at[i])
            for i, (far, near) in enumerate(((small_far, small), (cas_far, cas), (turn_far, turn)))
        ]
        load_x(0, 0).start()
        for copy in tables:
            copy.start()

        barrier = pltpu.get_barrier_semaphore()

        @pl.loop(1, n_left)
        def _(step):
            pl.semaphore_signal(barrier, inc=1, device_id={"left": partner(left, step)}, device_id_type=MESH)

        @pl.loop(1, n_right)
        def _(step):
            pl.semaphore_signal(barrier, inc=1, device_id={"right": right ^ step}, device_id_type=MESH)

        tables[0].wait()
        pl.semaphore_wait(barrier, n_left + n_right - 2)

        def product(slot, n):
            high, low = halves(taken[slot, :, n : n + 256])
            return dot(small[0], high) + dot(small[0], low) + dot(small[1], high)

        def send_half(y, h):
            to = left * part_y + y

            @pl.loop(1, n_left)
            def _(step):
                peer = partner(left, step)
                pltpu.make_async_remote_copy(
                    src_ref=held.at[y, pl.ds(peer * part_x + h * half_x, half_x)],
                    dst_ref=lines_y.at[to, pl.ds(h * half_x, half_x)],
                    send_sem=send_x,
                    recv_sem=recv_x.at[h],
                    device_id={"left": peer},
                    device_id_type=MESH,
                ).start()

            pltpu.make_async_copy(
                held.at[y, pl.ds(left * part_x + h * half_x, half_x)],
                lines_y.at[to, pl.ds(h * half_x, half_x)],
                keep_x.at[h],
            ).start()

        @pl.loop(0, part_y)
        def _(y):
            slot = y & 1

            @pl.when(y + 1 < part_y)
            def _():
                load_x(y + 1, 1 - slot).start()

            load_x(y, slot).wait()
            for n in range(0, part_z, 256):
                held[y, :, n : n + 256] = product(slot, n)
            send_half(y, 0)

        @pl.loop(0, part_y)
        def _(y):
            send_half(y, 1)

        tables[1].wait()
        tables[2].wait()

        @pl.loop(0, size_z // inner)
        def _(outer):
            cos = turn[0, pl.ds(outer, 1), :]
            sin = turn[1, pl.ds(outer, 1), :]
            for c in range(0, size_z, LANES):
                value = cas[0, :, c : c + LANES] * cos + cas[1, :, c : c + LANES] * sin
                high, low = halves(value)
                big_high[pl.ds(outer * inner, inner), c : c + LANES] = high
                big_low[pl.ds(outer * inner, inner), c : c + LANES] = low

        rows = pl.multiple_of(right * rows_y, rows_y)
        column[...] = jnp.broadcast_to(sym_y[:, pl.ds(rows, rows_y)], (rows_y, rows_y)).T

        def arrived_x(h):
            part = pl.ds(h * half_x, half_x)
            own = lines_y.at[pl.ds(0, part_y), part]
            pltpu.make_async_copy(own, own, keep_x.at[h]).wait()
            others = lines_y.at[pl.ds(0, size_y - part_y), part]
            pltpu.make_async_copy(others, others, recv_x.at[h]).wait()

        def load_y(k, slot):
            return pltpu.make_async_copy(lines_y.at[:, k, :], taken.at[slot], load_sem.at[slot])

        columns = pl.ds(pl.multiple_of(right * part_z, part_z), part_z)

        def send_plane(k):
            for flip, sem in ((2, far_y), (3, far_y), (1, near_y)):
                peer = right ^ flip
                pltpu.make_async_remote_copy(
                    src_ref=result.at[k, :, pl.ds(pl.multiple_of(peer * part_z, part_z), part_z)],
                    dst_ref=lines_z.at[k, :, columns],
                    send_sem=send_y.at[k],
                    recv_sem=sem.at[k],
                    device_id={"right": peer},
                    device_id_type=MESH,
                ).start()
            pltpu.make_async_copy(result.at[k, :, columns], lines_z.at[k, :, columns], keep_y.at[k]).start()

        def transform_y(first, last, send):
            load_y(first, first & 1).start()

            @pl.loop(first, last)
            def _(k):
                slot = k & 1

                @pl.when(k + 1 < last)
                def _():
                    load_y(k + 1, 1 - slot).start()

                load_y(k, slot).wait()
                for n in range(0, part_z, 256):
                    value = product(slot, n)
                    for r in range(n_right):
                        result[k, :, r * part_z + n : r * part_z + n + 256] = value[r * rows_y : (r + 1) * rows_y]
                if send:
                    send_plane(k)

        arrived_x(0)
        transform_y(0, half_x, False)
        arrived_x(1)

        @pl.loop(0, half_x)
        def _(k):
            send_plane(k)

        transform_y(half_x, part_x, True)

        here = pl.multiple_of((right >> 1) * half_z, half_z)
        there = pl.multiple_of(half_z - here, half_z)

        def line(k, side, start):
            return pltpu.make_async_copy(lines_z.at[k, :, pl.ds(start, half_z)], line_in.at[side], line_sem.at[side])

        def stack(side):
            high, low = halves(line_in[side])
            stacked[side, :rows_y] = high
            stacked[side, rows_y:] = low

        def product_z(side, start, cut):
            both = dot(stacked[side], big_high[pl.ds(start, half_z), cut])
            return both[:rows_y] + both[rows_y:] + dot(stacked[side, :rows_y], big_low[pl.ds(start, half_z), cut])

        @pl.loop(0, part_x)
        def _(k):
            mine = lines_z.at[k, :, pl.ds(0, part_z)]
            pltpu.make_async_copy(mine, mine, keep_y.at[k]).wait()
            pltpu.make_async_copy(mine, mine, near_y.at[k]).wait()
            line(k, 0, here).start()
            line(k, 0, here).wait()
            stack(0)

            @pl.loop(0, size_z, step=512)
            def _(n):
                cut = pl.ds(pl.multiple_of(n, 512), 512)
                partial[:, cut] = product_z(0, here, cut)

            theirs = lines_z.at[k, :, pl.ds(0, half_z)]
            pltpu.make_async_copy(theirs, theirs, far_y.at[k]).wait()
            line(k, 1, there).start()
            sent = lines_z.at[k, :, pl.ds(0, size_z - part_z)]
            pltpu.make_async_copy(sent, sent, send_y.at[k]).wait()
            line(k, 1, there).wait()
            stack(1)
            sym_xy = sym_x[left * part_x + k] + column[...]

            @pl.loop(0, size_z, step=512)
            def _(n):
                cut = pl.ds(pl.multiple_of(n, 512), 512)
                total = partial[:, cut] + product_z(1, there, cut)
                for c in range(0, 512, LANES):
                    some = pl.ds(pl.multiple_of(n + c, LANES), LANES)
                    result[k, :, some] = total[:, c : c + LANES] * lax.rsqrt(sym_xy + sym_z[:, some])

        others = lines_y.at[pl.ds(0, size_y - part_y)]
        pltpu.make_async_copy(others, others, send_x).wait()

    far = pl.BlockSpec(memory_space=pltpu.HBM)
    inside = pl.BlockSpec(memory_space=pltpu.VMEM)
    dma = pltpu.SemaphoreType.DMA
    return pl.pallas_call(
        kernel,
        out_shape=[
            jax.ShapeDtypeStruct((size_y, part_x, part_z), F32),
            jax.ShapeDtypeStruct((part_x, rows_y, size_z), F32),
            pltpu.VMEM((part_x, rows_y, size_z), F32),
        ],
        in_specs=[far] * 4 + [pl.BlockSpec(memory_space=pltpu.SMEM), inside, inside],
        out_specs=[far, far, inside],
        scratch_shapes=[
            pltpu.VMEM((part_y, size_x, part_z), F32),
            pltpu.VMEM((size_z, size_z), BF16),
            pltpu.VMEM((size_z, size_z), BF16),
            pltpu.VMEM((2, size_x, part_z), F32),
            pltpu.VMEM((2, rows_y, half_z), F32),
            pltpu.VMEM((2, 2 * rows_y, half_z), BF16),
            pltpu.VMEM((rows_y, size_z), F32),
            pltpu.VMEM((2, size_x, size_x), BF16),
            pltpu.VMEM((2, inner, size_z), F32),
            pltpu.VMEM((2, size_z // inner, LANES), F32),
            pltpu.VMEM((rows_y, rows_y), F32),
            dma((2,)), dma((3,)),
            dma, dma((2,)), dma((2,)),
            dma((part_x,)), dma((part_x,)), dma((part_x,)), dma((part_x,)),
            dma((2,)),
        ],
        compiler_params=pltpu.CompilerParams(
            collective_id=0, has_side_effects=True, vmem_limit_bytes=46 * 1024 * 1024
        ),
        name="hartley",
    )


def solution(mesh):
    n_left, n_right = mesh.shape["left"], mesh.shape["right"]

    def per_device(density, symbol_x, symbol_y, symbol_z):
        size_x, size_y, size_z = density.shape[0], density.shape[1] * n_left, density.shape[2] * n_right
        small = jnp.asarray(small_table(size_x))
        cas, turn = (jnp.asarray(t) for t in factor_tables(size_z, 64))
        kernel = make_kernel(n_left, n_right, size_x, size_y, size_z)
        return kernel(density, small, cas, turn, symbol_x, symbol_y[None, :], symbol_z[None, :])[2]

    return jax.shard_map(
        per_device,
        mesh=mesh,
        in_specs=(P(None, "left", "right"), P(), P(), P()),
        out_specs=P("left", "right", None),
        check_vma=False,
    )
```

time: 404 us -> 387 us (0.958)
  other arithmetic: 12.1 us -> 0 us
  Pallas kernels: 385 us -> 379 us
  local copies, waits for them, and re-layouts: 1.52 us -> 6.16 us
    mul x1 -> x0, other arithmetic: 12 us -> none  [per_device(): return result * lax.rsqrt(symbol)]
    unnamed x2 -> x1, local copies, waits for them, and re-layouts: 0.01 us -> 6.16 us
    pallas_call x1, Pallas kernels: 385 us -> 379 us  [per_device(): kernel(density, small, cas, turn, symbol_x, symbol_y[None, :], symbol_z[N...]
where the time goes in v2:
time: 387 us; the launch traced here: 385 us
  Pallas kernels  379 us (98%)
  local copies, waits for them, and re-layouts  6.16 us (2%)
    pallas_call x1, Pallas kernels, per_device(): kernel(density, small, cas, turn, symbol_x, symbol_y[None, :], symbol_z[N...  379 us

profile of v2, /device:TPU:1, one launch (start us, length us, event | category | flops | bytes accessed | tf_op | source)
XLA Modules:
  0.0 385.3 jit_solution(6909893488495479251)
XLA Ops:
  0.0 379.1 %hartley.1 = (f32[512,16,512]{2,1,0:T(8,128)}, f32[16,128,2048]{2,1,0:T(8,128)}, f32[16,128,2048]{2,1,0:T(8,128)S(1)}) custom-call(f32[512,16,512]{2,1,0:T(8,128)} %field.1, bf16[2,512,512]{2,1,0:T(8,128)(2,1)} %constant.6.clone.small_far, f32[2,64,2048]{2,1,0:T(8,128)} %constant.7.clone.cas_far, f32[2,32,128]{2,1,0:T(8,128)} %constant.8.clone.turn_far, ...), custom_call_target="tpu_custom_call" | custom-call | tf_op jit(solution)/shard_map/hartley/pallas_call | solution.py:294
  379.1 6.2 %copy.9 = f32[16,128,2048]{2,1,0:T(8,128)} copy(f32[16,128,2048]{2,1,0:T(8,128)S(1)} %get-tuple-element.6) | data formatting | bytes 33554432

commit v3 on v2

--- a/solution.py
+++ b/solution.py
@@ -44,6 +44,7 @@
 def make_kernel(n_left, n_right, size_x, size_y, size_z):
     part_x, part_y, rows_y, part_z = size_x // n_left, size_y // n_left, size_y // n_right, size_z // n_right
     half_x, half_z = part_x // 2, size_z // 2
+    last_y = max(1, part_y // 4)
     inner = 64
 
     def partner(me, step):
@@ -90,7 +91,7 @@
             high, low = halves(taken[slot, :, n : n + 256])
             return dot(small[0], high) + dot(small[0], low) + dot(small[1], high)
 
-        def send_half(y, h):
+        def send_half(y, h, sem):
             to = left * part_y + y
 
             @pl.loop(1, n_left)
@@ -99,7 +100,7 @@
                 pltpu.make_async_remote_copy(
                     src_ref=held.at[y, pl.ds(peer * part_x + h * half_x, half_x)],
                     dst_ref=lines_y.at[to, pl.ds(h * half_x, half_x)],
-                    send_sem=send_x,
+                    send_sem=send_x.at[sem],
                     recv_sem=recv_x.at[h],
                     device_id={"left": peer},
                     device_id_type=MESH,
@@ -122,11 +123,19 @@
             load_x(y, slot).wait()
             for n in range(0, part_z, 256):
                 held[y, :, n : n + 256] = product(slot, n)
-            send_half(y, 0)
-
-        @pl.loop(0, part_y)
+            send_half(y, 0, 0)
+
+        @pl.loop(0, part_y - last_y)
         def _(y):
-            send_half(y, 1)
+            send_half(y, 1, 1)
+
+        @pl.loop(part_y - last_y, part_y)
+        def _(y):
+            send_half(y, 1, 2)
+
+        def left_x(sem, planes):
+            gone = lines_y.at[pl.ds(0, planes * (n_left - 1)), pl.ds(0, half_x)]
+            pltpu.make_async_copy(gone, gone, send_x.at[sem]).wait()
 
         tables[1].wait()
         tables[2].wait()
@@ -190,12 +199,15 @@
 
         arrived_x(0)
         transform_y(0, half_x, False)
-        arrived_x(1)
+
+        left_x(0, part_y)
+        left_x(1, part_y - last_y)
 
         @pl.loop(0, half_x)
         def _(k):
             send_plane(k)
 
+        arrived_x(1)
         transform_y(half_x, part_x, True)
 
         here = pl.multiple_of((right >> 1) * half_z, half_z)
@@ -244,8 +256,7 @@
                     some = pl.ds(pl.multiple_of(n + c, LANES), LANES)
                     result[k, :, some] = total[:, c : c + LANES] * lax.rsqrt(sym_xy + sym_z[:, some])
 
-        others = lines_y.at[pl.ds(0, size_y - part_y)]
-        pltpu.make_async_copy(others, others, send_x).wait()
+        left_x(2, last_y)
 
     far = pl.BlockSpec(memory_space=pltpu.HBM)
     inside = pl.BlockSpec(memory_space=pltpu.VMEM)
@@ -272,7 +283,7 @@
             pltpu.VMEM((2, size_z // inner, LANES), F32),
             pltpu.VMEM((rows_y, rows_y), F32),
             dma((2,)), dma((3,)),
-            dma, dma((2,)), dma((2,)),
+            dma((3,)), dma((2,)), dma((2,)),
             dma((part_x,)), dma((part_x,)), dma((part_x,)), dma((part_x,)),
             dma((2,)),
         ],

time: 387 us -> 386 us (level)
  no operation moved by 1% of the time
where the time goes in v3:
time: 386 us; the launch traced here: 384 us
  Pallas kernels  378 us (98%)
  local copies, waits for them, and re-layouts  6.16 us (2%)
    pallas_call x1, Pallas kernels, per_device(): kernel(density, small, cas, turn, symbol_x, symbol_y[None, :], symbol_z[N...  378 us

profile of v3, /device:TPU:1, one launch (start us, length us, event | category | flops | bytes accessed | tf_op | source)
XLA Modules:
  0.0 383.7 jit_solution(18177798331546610964)
XLA Ops:
  0.0 377.6 %hartley.1 = (f32[512,16,512]{2,1,0:T(8,128)}, f32[16,128,2048]{2,1,0:T(8,128)}, f32[16,128,2048]{2,1,0:T(8,128)S(1)}) custom-call(f32[512,16,512]{2,1,0:T(8,128)} %field.1, bf16[2,512,512]{2,1,0:T(8,128)(2,1)} %constant.6.clone.small_far, f32[2,64,2048]{2,1,0:T(8,128)} %constant.7.clone.cas_far, f32[2,32,128]{2,1,0:T(8,128)} %constant.8.clone.turn_far, ...), custom_call_target="tpu_custom_call" | custom-call | tf_op jit(solution)/shard_map/hartley/pallas_call | solution.py:305
  377.6 6.2 %copy.9 = f32[16,128,2048]{2,1,0:T(8,128)} copy(f32[16,128,2048]{2,1,0:T(8,128)S(1)} %get-tuple-element.6) | data formatting | bytes 33554432

commit v4 on v3

--- a/solution.py
+++ b/solution.py
@@ -83,9 +83,6 @@
         @pl.loop(1, n_right)
         def _(step):
             pl.semaphore_signal(barrier, inc=1, device_id={"right": right ^ step}, device_id_type=MESH)
-
-        tables[0].wait()
-        pl.semaphore_wait(barrier, n_left + n_right - 2)
 
         def product(slot, n):
             high, low = halves(taken[slot, :, n : n + 256])
@@ -112,7 +109,15 @@
                 keep_x.at[h],
             ).start()
 
-        @pl.loop(0, part_y)
+        load_x(1, 1).start()
+        tables[0].wait()
+        load_x(0, 0).wait()
+        for n in range(0, part_z, 256):
+            held[0, :, n : n + 256] = product(0, n)
+        pl.semaphore_wait(barrier, n_left + n_right - 2)
+        send_half(0, 0, 0)
+
+        @pl.loop(1, part_y)
         def _(y):
             slot = y & 1
 
@@ -166,13 +171,13 @@
         columns = pl.ds(pl.multiple_of(right * part_z, part_z), part_z)
 
         def send_plane(k):
-            for flip, sem in ((2, far_y), (3, far_y), (1, near_y)):
+            for flip, sem in ((2, far_y.at[0, k]), (3, far_y.at[1, k]), (1, near_y.at[k])):
                 peer = right ^ flip
                 pltpu.make_async_remote_copy(
                     src_ref=result.at[k, :, pl.ds(pl.multiple_of(peer * part_z, part_z), part_z)],
                     dst_ref=lines_z.at[k, :, columns],
                     send_sem=send_y.at[k],
-                    recv_sem=sem.at[k],
+                    recv_sem=sem,
                     device_id={"right": peer},
                     device_id_type=MESH,
                 ).start()
@@ -210,48 +215,65 @@
         arrived_x(1)
         transform_y(half_x, part_x, True)
 
-        here = pl.multiple_of((right >> 1) * half_z, half_z)
-        there = pl.multiple_of(half_z - here, half_z)
-
-        def line(k, side, start):
-            return pltpu.make_async_copy(lines_z.at[k, :, pl.ds(start, half_z)], line_in.at[side], line_sem.at[side])
-
-        def stack(side):
-            high, low = halves(line_in[side])
-            stacked[side, :rows_y] = high
-            stacked[side, rows_y:] = low
-
-        def product_z(side, start, cut):
-            both = dot(stacked[side], big_high[pl.ds(start, half_z), cut])
-            return both[:rows_y] + both[rows_y:] + dot(stacked[side, :rows_y], big_low[pl.ds(start, half_z), cut])
+        here = (right >> 1) * half_z
+        pieces = (
+            (here, half_z, line_in.at[0], stacked.at[0]),
+            ((right ^ 2) * part_z, part_z, line_in.at[1, :, pl.ds(0, part_z)], stacked.at[1, :, pl.ds(0, part_z)]),
+            ((right ^ 3) * part_z, part_z, line_in.at[1, :, pl.ds(part_z, part_z)], stacked.at[1, :, pl.ds(part_z, part_z)]),
+        )
+
+        def line(k, piece):
+            start, depth, into, _ = pieces[piece]
+            part = pl.ds(pl.multiple_of(start, part_z), depth)
+            return pltpu.make_async_copy(lines_z.at[k, :, part], into, line_sem.at[piece])
+
+        def stack(piece):
+            high, low = halves(pieces[piece][2][...])
+            pieces[piece][3][:rows_y] = high
+            pieces[piece][3][rows_y:] = low
+
+        def product_z(piece, cut):
+            start, depth, _, both_halves = pieces[piece]
+            part = pl.ds(pl.multiple_of(start, part_z), depth)
+            both = dot(both_halves[...], big_high[part, cut])
+            return both[:rows_y] + both[rows_y:] + dot(both_halves[:rows_y], big_low[part, cut])
 
         @pl.loop(0, part_x)
         def _(k):
             mine = lines_z.at[k, :, pl.ds(0, part_z)]
             pltpu.make_async_copy(mine, mine, keep_y.at[k]).wait()
             pltpu.make_async_copy(mine, mine, near_y.at[k]).wait()
-            line(k, 0, here).start()
-            line(k, 0, here).wait()
+            line(k, 0).start()
+            line(k, 0).wait()
             stack(0)
 
             @pl.loop(0, size_z, step=512)
             def _(n):
                 cut = pl.ds(pl.multiple_of(n, 512), 512)
-                partial[:, cut] = product_z(0, here, cut)
-
-            theirs = lines_z.at[k, :, pl.ds(0, half_z)]
-            pltpu.make_async_copy(theirs, theirs, far_y.at[k]).wait()
-            line(k, 1, there).start()
-            sent = lines_z.at[k, :, pl.ds(0, size_z - part_z)]
-            pltpu.make_async_copy(sent, sent, send_y.at[k]).wait()
-            line(k, 1, there).wait()
+                partial[:, cut] = product_z(0, cut)
+
+            pltpu.make_async_copy(mine, mine, far_y.at[0, k]).wait()
+            line(k, 1).start()
+            line(k, 1).wait()
             stack(1)
-            sym_xy = sym_x[left * part_x + k] + column[...]
 
             @pl.loop(0, size_z, step=512)
             def _(n):
                 cut = pl.ds(pl.multiple_of(n, 512), 512)
-                total = partial[:, cut] + product_z(1, there, cut)
+                partial[:, cut] += product_z(1, cut)
+
+            pltpu.make_async_copy(mine, mine, far_y.at[1, k]).wait()
+            line(k, 2).start()
+            sent = lines_z.at[k, :, pl.ds(0, size_z - part_z)]
+            pltpu.make_async_copy(sent, sent, send_y.at[k]).wait()
+            line(k, 2).wait()
+            stack(2)
+            sym_xy = sym_x[left * part_x + k] + column[...]
+
+            @pl.loop(0, size_z, step=512)
+            def _(n):
+                cut = pl.ds(pl.multiple_of(n, 512), 512)
+                total = partial[:, cut] + product_z(2, cut)
                 for c in range(0, 512, LANES):
                     some = pl.ds(pl.multiple_of(n + c, LANES), LANES)
                     result[k, :, some] = total[:, c : c + LANES] * lax.rsqrt(sym_xy + sym_z[:, some])
@@ -284,8 +306,8 @@
             pltpu.VMEM((rows_y, rows_y), F32),
             dma((2,)), dma((3,)),
             dma((3,)), dma((2,)), dma((2,)),
-            dma((part_x,)), dma((part_x,)), dma((part_x,)), dma((part_x,)),
-            dma((2,)),
+            dma((part_x,)), dma((part_x,)), dma((2, part_x)), dma((part_x,)),
+            dma((3,)),
         ],
         compiler_params=pltpu.CompilerParams(
             collective_id=0, has_side_effects=True, vmem_limit_bytes=46 * 1024 * 1024

time: 386 us -> 384 us (level)
  no operation moved by 1% of the time
where the time goes in v4:
time: 384 us; the launch traced here: 382 us
  Pallas kernels  376 us (98%)
  local copies, waits for them, and re-layouts  6.16 us (2%)
    pallas_call x1, Pallas kernels, per_device(): kernel(density, small, cas, turn, symbol_x, symbol_y[None, :], symbol_z[N...  376 us

profile of v4, /device:TPU:1, one launch (start us, length us, event | category | flops | bytes accessed | tf_op | source)
XLA Modules:
  0.0 381.7 jit_solution(12821260646113744163)
XLA Ops:
  0.0 375.5 %hartley.1 = (f32[512,16,512]{2,1,0:T(8,128)}, f32[16,128,2048]{2,1,0:T(8,128)}, f32[16,128,2048]{2,1,0:T(8,128)S(1)}) custom-call(f32[512,16,512]{2,1,0:T(8,128)} %field.1, bf16[2,512,512]{2,1,0:T(8,128)(2,1)} %constant.6.clone.small_far, f32[2,64,2048]{2,1,0:T(8,128)} %constant.7.clone.cas_far, f32[2,32,128]{2,1,0:T(8,128)} %constant.8.clone.turn_far, ...), custom_call_target="tpu_custom_call" | custom-call | tf_op jit(solution)/shard_map/hartley/pallas_call | solution.py:327
  375.5 6.2 %copy.9 = f32[16,128,2048]{2,1,0:T(8,128)} copy(f32[16,128,2048]{2,1,0:T(8,128)S(1)} %get-tuple-element.6) | data formatting | bytes 33554432

commit v5 on v4

--- a/solution.py
+++ b/solution.py
@@ -44,7 +44,7 @@
 def make_kernel(n_left, n_right, size_x, size_y, size_z):
     part_x, part_y, rows_y, part_z = size_x // n_left, size_y // n_left, size_y // n_right, size_z // n_right
     half_x, half_z = part_x // 2, size_z // 2
-    last_y = max(1, part_y // 4)
+    last_y = max(1, part_y // 2)
     inner = 64
 
     def partner(me, step):

time: 384 us -> 384 us (level)
  no operation moved by 1% of the time
where the time goes in v5:
time: 384 us; the launch traced here: 382 us
  Pallas kernels  376 us (98%)
  local copies, waits for them, and re-layouts  6.16 us (2%)
    pallas_call x1, Pallas kernels, per_device(): kernel(density, small, cas, turn, symbol_x, symbol_y[None, :], symbol_z[N...  376 us

profile of v5, /device:TPU:1, one launch (start us, length us, event | category | flops | bytes accessed | tf_op | source)
XLA Modules:
  0.0 381.7 jit_solution(2790601362490031359)
XLA Ops:
  0.0 375.5 %hartley.1 = (f32[512,16,512]{2,1,0:T(8,128)}, f32[16,128,2048]{2,1,0:T(8,128)}, f32[16,128,2048]{2,1,0:T(8,128)S(1)}) custom-call(f32[512,16,512]{2,1,0:T(8,128)} %field.1, bf16[2,512,512]{2,1,0:T(8,128)(2,1)} %constant.6.clone.small_far, f32[2,64,2048]{2,1,0:T(8,128)} %constant.7.clone.cas_far, f32[2,32,128]{2,1,0:T(8,128)} %constant.8.clone.turn_far, ...), custom_call_target="tpu_custom_call" | custom-call | tf_op jit(solution)/shard_map/hartley/pallas_call | solution.py:327
  375.5 6.2 %copy.9 = f32[16,128,2048]{2,1,0:T(8,128)} copy(f32[16,128,2048]{2,1,0:T(8,128)S(1)} %get-tuple-element.6) | data formatting | bytes 33554432
